TPU v7x, 32 devices: a whole 2x2x4 slice. The times are simulated.
32 devices in a mesh: dp: 4 (over x, core), vocab: 8 (over z, y).
Axes of the slice: x: 2, y: 2, z: 4, core: 2. Of those that a mesh axis runs over, the one named last changes fastest.
Arguments:
- policy_hidden: bfloat16 [512, 4096], P('dp'), may hold values from -84 to 84
- policy_weight: bfloat16 [4096, 65536], P('dp', 'vocab'), may hold values from -0.09375 to 0.09375
- reference_hidden: bfloat16 [512, 4096], P(('dp', 'vocab')), may hold values from -84 to 84
- reference_weight: bfloat16 [4096, 65536], P(None, ('dp', 'vocab')), may hold values from -0.09375 to 0.09375
- targets: int32 [512], replicated, may hold values from 0 to 65535
- response_mask: int32 [512], replicated, may hold values 0 or 1
- pair_index: int32 [16], replicated, may hold values from 0 to 15, each once
Outputs:
- hidden_grad: bfloat16 [512, 4096], P('vocab', 'dp')
- weight_grad: bfloat16 [4096, 65536], P('dp', 'vocab')
- total_loss: float32 [], replicated
Inputs may be any that keep to these rules, and one draw needn't show every extreme that they name: `pair_index`: each number of 0 to 15 once; entries 2p and 2p + 1 are the chosen and the rejected sequence of pair p.
All inputs are finite; a program needn't handle non-finite values.
Results may differ from a plain program's by a relative error of at most 0.005.
The roundings to bfloat16 on the way count: a program that leaves them out, or rounds other values in their place, can miss the bound.
Values may be sent and summed in bfloat16 or wider, within the bound.
A program may use at most 128 MiB of HBM per device.

v0:
```python
import functools

import jax
import jax.numpy as jnp
from jax import lax
from jax.experimental import pallas as pl
from jax.experimental.pallas import tpu as pltpu
from jax.sharding import PartitionSpec as P

SEQ_LEN = 32


beta = 0.1
loss_scale = 4096.0


def pair_terms(log_ratio, pair_index):
    chosen = pair_index[0::2]
    rejected = pair_index[1::2]
    margin = beta * (log_ratio[chosen] - log_ratio[rejected])
    pair_count = chosen.shape[0]
    total_loss = jnp.sum(jax.nn.softplus(-margin)) / pair_count
    weight = -beta * loss_scale * jax.nn.sigmoid(-margin) / pair_count
    numbers = jnp.arange(log_ratio.shape[0], dtype=jnp.int32)[:, None]
    factor = jnp.sum(
        jnp.where(numbers == chosen[None, :], weight[None, :], 0.0)
        - jnp.where(numbers == rejected[None, :], weight[None, :], 0.0),
        axis=1,
    )
    return (total_loss, factor)


def local_pick(logits, targets, offset, axis):
    column_ids = lax.broadcasted_iota(jnp.int32, logits.shape, axis)
    shifted = targets - offset
    wanted = shifted[:, None]
    return jnp.sum(jnp.where(column_ids == wanted, logits, 0.0), axis=axis)


def gather_kernel(nd, nv, x_ref, out_ref, own_sem, send_d, recv_d, send_v, recv_v):
    d, v = lax.axis_index("dp"), lax.axis_index("vocab")
    data_peers = [lax.rem(d + k, nd) for k in range(1, nd)]
    vocab_peers = [lax.rem(v + k, nv) for k in range(1, nv)]
    barrier = pltpu.get_barrier_semaphore()
    for peer in data_peers:
        pl.semaphore_signal(
            barrier, inc=1, device_id=(peer, v), device_id_type=pl.DeviceIdType.MESH
        )
    for peer in vocab_peers:
        pl.semaphore_signal(
            barrier, inc=1, device_id=(d, peer), device_id_type=pl.DeviceIdType.MESH
        )
    pl.semaphore_wait(barrier, nd + nv - 2)
    own = pltpu.make_async_copy(x_ref, out_ref.at[v, d], own_sem)
    own.start()
    copies = [
        pltpu.make_async_remote_copy(
            src_ref=x_ref,
            dst_ref=out_ref.at[v, d],
            send_sem=send_d.at[k],
            recv_sem=recv_d.at[k],
            device_id=(peer, v),
            device_id_type=pl.DeviceIdType.MESH,
        )
        for k, peer in enumerate(data_peers)
    ]
    for copy in copies:
        copy.start()
    own.wait()
    for copy in copies:
        copy.wait()
    copies = [
        pltpu.make_async_remote_copy(
            src_ref=out_ref.at[v],
            dst_ref=out_ref.at[v],
            send_sem=send_v.at[k],
            recv_sem=recv_v.at[k],
            device_id=(d, peer),
            device_id_type=pl.DeviceIdType.MESH,
        )
        for k, peer in enumerate(vocab_peers)
    ]
    for copy in copies:
        copy.start()
    for copy in copies:
        copy.wait()


def gather_stats(stats):
    nd, nv = lax.axis_size("dp"), lax.axis_size("vocab")
    size = stats.shape[0]
    rows = -(-size // 1024) * 8
    stats = jnp.pad(stats, (0, rows * 128 - size)).reshape(rows, 128)
    gathered = pl.pallas_call(
        functools.partial(gather_kernel, nd, nv),
        out_shape=jax.ShapeDtypeStruct((nv, nd, rows, 128), jnp.float32),
        in_specs=[pl.BlockSpec(memory_space=pltpu.VMEM)],
        out_specs=pl.BlockSpec(memory_space=pltpu.VMEM),
        scratch_shapes=[
            pltpu.SemaphoreType.DMA,
            pltpu.SemaphoreType.DMA((nd - 1,)),
            pltpu.SemaphoreType.DMA((nd - 1,)),
            pltpu.SemaphoreType.DMA((nv - 1,)),
            pltpu.SemaphoreType.DMA((nv - 1,)),
        ],
        compiler_params=pltpu.CompilerParams(collective_id=0, has_side_effects=True),
        name="gather_stats",
    )(stats)
    return gathered.reshape(nv, nd, rows * 128)[:, :, :size]


def grad_kernel(rows_ref, segment_ref, out_ref):
    out_ref[...] = jnp.dot(
        rows_ref[...], segment_ref[...], preferred_element_type=jnp.float32
    ).astype(out_ref.dtype)


def grad_matmul(rows, segment):
    depth, tokens = rows.shape
    width = segment.shape[1]
    tile = 512 if width % 512 == 0 else width
    return pl.pallas_call(
        grad_kernel,
        grid=(width // tile,),
        in_specs=[
            pl.BlockSpec((depth, tokens), lambda i: (0, 0)),
            pl.BlockSpec((tokens, tile), lambda i: (0, i)),
        ],
        out_specs=pl.BlockSpec((depth, tile), lambda i: (0, i)),
        out_shape=jax.ShapeDtypeStruct((depth, width), jnp.bfloat16),
        cost_estimate=pl.CostEstimate(
            flops=2 * depth * tokens * width,
            bytes_accessed=2 * (depth * tokens + tokens * width + depth * width),
            transcendentals=0,
        ),
        name="weight_grad",
    )(rows, segment)


def local(
    policy_hidden,
    policy_weight,
    reference_hidden,
    reference_weight,
    targets,
    response_mask,
    pair_index,
):
    data_index = lax.axis_index("dp")
    vocab_index = lax.axis_index("vocab")
    vocab_devices = lax.axis_size("vocab")
    local_tokens = policy_hidden.shape[0]
    policy_width = policy_weight.shape[1]
    reference_width = reference_weight.shape[1]
    active = response_mask.astype(jnp.float32)
    columns = lax.all_to_all(policy_hidden, "dp", split_axis=1, concat_axis=0, tiled=True)
    reference_logits = jnp.dot(
        lax.all_gather(reference_hidden, ("dp", "vocab"), axis=0, tiled=True),
        reference_weight,
        preferred_element_type=jnp.float32,
    )
    reference_offset = (data_index * vocab_devices + vocab_index) * reference_width
    reference_top = jnp.max(reference_logits, axis=1)
    reference_sum = jnp.sum(jnp.exp(reference_logits - reference_top[:, None]), axis=1)
    reference_pick = local_pick(reference_logits, targets, reference_offset, 1)
    policy_logits = lax.psum_scatter(
        jnp.dot(columns, policy_weight, preferred_element_type=jnp.float32),
        "dp",
        scatter_dimension=0,
        tiled=True,
    )
    own_targets = lax.dynamic_slice_in_dim(targets, data_index * local_tokens, local_tokens, 0)
    policy_offset = vocab_index * policy_width
    policy_pick = local_pick(policy_logits, own_targets, policy_offset, 1)
    policy_top = jnp.max(policy_logits, axis=1)
    policy_sum = jnp.sum(jnp.exp(policy_logits - policy_top[:, None]), axis=1)
    stats = jnp.concatenate(
        [policy_top, policy_sum, policy_pick, reference_top, reference_sum, reference_pick]
    )
    stats = gather_stats(stats)
    tokens = targets.shape[0]
    policy_stats = stats[:, :, : 3 * local_tokens].reshape(vocab_devices, -1, 3, local_tokens)
    policy_max = jnp.max(policy_stats[:, :, 0], axis=0)
    policy_scaled = policy_stats[:, :, 1] * jnp.exp(policy_stats[:, :, 0] - policy_max[None])
    policy_totals = (policy_max + jnp.log(jnp.sum(policy_scaled, axis=0))).reshape(tokens)
    policy_logp = jnp.sum(policy_stats[:, :, 2], axis=0).reshape(tokens) - policy_totals
    reference_stats = stats[:, :, 3 * local_tokens :].reshape(-1, 3, tokens)
    reference_max = jnp.max(reference_stats[:, 0], axis=0)
    reference_scaled = reference_stats[:, 1] * jnp.exp(reference_stats[:, 0] - reference_max[None])
    reference_logp = (
        jnp.sum(reference_stats[:, 2], axis=0)
        - reference_max
        - jnp.log(jnp.sum(reference_scaled, axis=0))
    )
    log_ratio = jnp.sum((active * (policy_logp - reference_logp)).reshape(-1, SEQ_LEN), axis=1)
    total_loss, factor = pair_terms(log_ratio, pair_index)
    token_scale = lax.dynamic_slice_in_dim(
        active * jnp.repeat(factor, SEQ_LEN), data_index * local_tokens, local_tokens, 0
    )
    policy_total = lax.dynamic_slice_in_dim(
        policy_totals, data_index * local_tokens, local_tokens, 0
    )
    column_ids = lax.broadcasted_iota(jnp.int32, policy_logits.shape, 1)
    onehot = (column_ids == (own_targets - policy_offset)[:, None]).astype(jnp.float32)
    logit_grad = (
        token_scale[:, None] * (onehot - jnp.exp(policy_logits - policy_total[:, None]))
    ).astype(jnp.bfloat16)
    segment = lax.all_gather(logit_grad, "dp", axis=0, tiled=True)
    hidden_piece = lax.dot_general(
        segment, policy_weight, (((1,), (1,)), ((), ())), preferred_element_type=jnp.float32
    )
    pieces = lax.all_to_all(
        hidden_piece.astype(jnp.bfloat16).reshape(vocab_devices, -1, hidden_piece.shape[1]),
        "vocab",
        split_axis=0,
        concat_axis=0,
    )
    hidden_grad = jnp.sum(pieces.astype(jnp.float32), axis=0)
    weight_grad = grad_matmul(columns.T, segment)
    return (hidden_grad.astype(jnp.bfloat16), weight_grad, total_loss)


def solution(mesh):
    placed = (
        P("dp", None),
        P("dp", "vocab"),
        P(("dp", "vocab"), None),
        P(None, ("dp", "vocab")),
        P(),
        P(),
        P(),
    )
    return jax.shard_map(
        local,
        mesh=mesh,
        in_specs=placed,
        out_specs=(P("vocab", "dp"), P("dp", "vocab"), P()),
        check_vma=False,
    )
```

profile of v0, /device:TPU:0, one launch (start us, length us, event | category | flops | bytes accessed | tf_op | source)
XLA Modules:
  0.0 317.8 jit_solution(3243412504919556975)
XLA Ops:
  8.0 0.0 all-gather.3.cloned.1.call-start
  8.0 0.7 all-gather.3.cloned.1.call-update
  8.7 0.0 reduce-scatter.2.cloned.1.call-start
  8.8 1.6 copy.22
  10.4 19.4 %all_to_all.24 = bf16[128,4,1024]{0,2,1:T(8,128)(2,1)S(1)} all-to-all(bf16[128,4,1024]{0,2,1:T(8,128)(2,1)S(1)} %bitcast.51), channel_id=1, replica_groups=mesh['dp'=4,'vocab'=8] {'dp'}, dimensions={1} | all-to-all | bytes 2097152 | tf_op jit(solution)/shard_map/all_to_all | solution.py:156
  29.8 16.0 %fusion = f32[512,8192]{1,0:T(8,128)} fusion(bf16[1024,8192]{1,0:T(8,128)(2,1)} %param.8, bf16[128,4,1024]{0,2,1:T(8,128)(2,1)S(1)} %all_to_all.24), kind=kOutput, calls=%fused_computation.11 | convolution fusion | flops 8589934592 | bytes 34603008 | tf_op jit(solution)/shard_map/dot_general | solution.py:167
  45.8 0.0 copy-start.2
  45.8 0.0 copy-start.1
  45.8 0.0 reduce-scatter.2.cloned.1.call-update
  45.8 0.2 all-gather.5.cloned.1.call-start
  46.1 0.4 copy-done.2
  46.5 0.1 slice.35
  46.5 0.1 slice.44
  46.6 0.0 copy-done.1
  46.6 0.1 dynamic-slice_subtract_fusion
  46.8 30.1 %all-gather.3.cloned.1.call-done = bf16[512,4096]{1,0:T(8,128)(2,1)} async-done(((bf16[16,4096]{1,0:T(8,128)(2,1)}), bf16[512,4096]{1,0:T(8,128)(2,1)}) %all-gather.3.cloned.1.call-update) | async-done | bytes 4194320 | tf_op jit(solution)/shard_map/all_gather | solution.py:158
  76.9 13.8 %fusion.11 = (f32[512]{0:T(512)S(1)}, f32[512,2048]{1,0:T(8,128)S(1)}) fusion(bf16[512,4096]{1,0:T(8,128)(2,1)} %all-gather.3.cloned.1.call-done, bf16[4096,2048]{1,0:T(8,128)(2,1)} %param.10), kind=kOutput, calls=%fused_computation.49 | convolution fusion | flops 8590983168 | bytes 25167872 | tf_op jit(solution)/shard_map/dot_general | solution.py:157
  90.7 1.4 select_reduce_fusion
  92.1 80.1 %reduce-scatter.2.cloned.1.call-done = f32[128,8192]{1,0:T(8,128)} async-done(((f32[512,8192]{1,0:T(8,128)}), f32[128,8192]{1,0:T(8,128)}) %reduce-scatter.2.cloned.1.call-update) | async-done | bytes 4194320 | tf_op jit(solution)/shard_map/reduce_scatter | solution.py:166
  172.2 2.5 reduce_max.36
  174.7 0.0 copy-start
  174.7 3.4 %select_reduce_fusion.1 = (f32[128]{0:T(128)S(1)}, f32[128]{0:T(128)S(1)}) fusion(f32[128,8192]{1,0:T(8,128)} %reduce-scatter.2.cloned.1.call-done, s32[128]{0:T(128)S(1)} %dynamic-slice_subtract_fusion, f32[128]{0:T(128)S(1)} %reduce_max.36), kind=kLoop, calls=%fused_computation.6 | loop fusion | flops 5242624 | bytes 4196352 | tf_op jit(solution)/shard_map/reduce_sum | solution.py:37
  178.2 0.6 pad_bitcast_fusion.x_ref
  178.8 13.4 %gather_stats.1 = f32[8,4,16,128]{3,2,1,0:T(8,128)} custom-call(f32[16,128]{1,0:T(8,128)} %pad_bitcast_fusion.x_ref), custom_call_target="tpu_custom_call" | custom-call | tf_op jit(solution)/shard_map/gather_stats/pallas_call | solution.py:94
  192.2 1.0 reshape.59
  193.3 0.1 fusion.10
  193.4 0.2 reshape.62
  193.6 0.2 slice_reduce_fusion
  193.8 0.0 copy-done
  193.8 0.1 reshape.63
  193.9 0.1 reduce_sum.119
  194.0 0.6 gather_fusion
  194.7 0.6 gather_fusion.1
  195.3 0.6 fusion.9
  196.0 0.1 subtract_reduce_fusion
  196.0 0.1 broadcast_in_dim.53
  196.1 0.1 reshape.64
  196.2 0.1 dynamic_slice.10
  196.3 0.1 dynamic_slice.11
  196.4 4.7 %multiply_convert_fusion = bf16[128,8192]{1,0:T(8,128)(2,1)} fusion(f32[128,8192]{1,0:T(8,128)} %reduce-scatter.2.cloned.1.call-done, f32[128]{0:T(128)S(1)} %dynamic_slice.11, f32[128]{0:T(128)S(1)} %dynamic_slice.10, s32[128]{0:T(128)S(1)} %dynamic-slice_subtract_fusion), kind=kLoop, calls=%fused_computation.2 | loop fusion | flops 6291456 | bytes 6292992 | tf_op jit(solution)/shard_map/convert_element_type | solution.py:207
  201.1 0.0 all-gather.5.cloned.1.call-update
  201.1 59.9 %all-gather.5.cloned.1.call-done.segment_ref = bf16[512,8192]{1,0:T(8,128)(2,1)} async-done(((bf16[128,8192]{1,0:T(8,128)(2,1)}), bf16[512,8192]{1,0:T(8,128)(2,1)}) %all-gather.5.cloned.1.call-update) | async-done | bytes 8388624 | tf_op jit(solution)/shard_map/all_gather | solution.py:208
  261.0 15.7 %convolution_convert_fusion = bf16[512,1024]{1,0:T(8,128)(2,1)} fusion(bf16[512,8192]{1,0:T(8,128)(2,1)} %all-gather.5.cloned.1.call-done.segment_ref, bf16[1024,8192]{1,0:T(8,128)(2,1)} %param.8), kind=kOutput, calls=%fused_computation.9 | convolution fusion | flops 8590458880 | bytes 26214400 | tf_op jit(solution)/shard_map/dot_general | solution.py:209
  276.7 5.5 %all-to-all-start.1 = ((bf16[8,64,1024]{2,1,0:T(8,128)(2,1)}), bf16[8,64,1024]{2,1,0:T(8,128)(2,1)S(1)}, u32[]{:S(2)}, u32[]{:S(2)}) async-start(bf16[8,64,1024]{2,1,0:T(8,128)(2,1)} %bitcast.8), calls=%async_computation.2 | async-start | bytes 2097152 | tf_op jit(solution)/shard_map/all_to_all | solution.py:212
  282.2 1.1 bitcast_bitcast_fusion.rows_ref
  284.0 19.0 %weight_grad.1 = bf16[1024,8192]{1,0:T(8,128)(2,1)} custom-call(bf16[1024,512]{1,0:T(8,128)(2,1)} %bitcast_bitcast_fusion.rows_ref, bf16[512,8192]{1,0:T(8,128)(2,1)} %all-gather.5.cloned.1.call-done.segment_ref), custom_call_target="tpu_custom_call" | custom-call | flops 8589934592 | bytes 26214400 | tf_op jit(solution)/shard_map/weight_grad/pallas_call | solution.py:122
  302.9 5.5 %all-to-all-done.1 = bf16[8,64,1024]{2,1,0:T(8,128)(2,1)S(1)} async-done(((bf16[8,64,1024]{2,1,0:T(8,128)(2,1)}), bf16[8,64,1024]{2,1,0:T(8,128)(2,1)S(1)}, u32[]{:S(2)}, u32[]{:S(2)}) %all-to-all-start.1) | async-done | bytes 1048608 | tf_op jit(solution)/shard_map/all_to_all | solution.py:212
  308.4 0.8 reduce_sum.121
  (21 shorter events, 0.2 us)
Async XLA Ops:
  8.0 68.9 %all-gather.3.cloned.1.call-start = ((), (), s32[]{:S(2)}) async-start(), calls=%async_computation.4 | async-start | bytes 4325376 | tf_op jit(solution)/shard_map/all_gather | solution.py:158
  8.7 163.5 %reduce-scatter.2.cloned.1.call-start = ((), (), s32[]{:S(2)}) async-start(), calls=%async_computation.3 | async-start | bytes 20971520 | tf_op jit(solution)/shard_map/reduce_scatter | solution.py:166
  45.8 0.7 copy-start.2
  45.8 0.8 copy-start.1
  45.8 215.2 %all-gather.5.cloned.1.call-start = ((), (), s32[]{:S(2)}) async-start(), calls=%async_computation.5 | async-start | bytes 10485760 | tf_op jit(solution)/shard_map/all_gather | solution.py:208
  174.7 19.1 %copy-start = (s32[512]{0:T(512)S(1)}, s32[512]{0:T(512)}, u32[]{:S(2)}) copy-start(s32[512]{0:T(512)} %param.12) | copy-start | bytes 6148
  276.7 31.7 %all-to-all-start.1 = ((bf16[8,64,1024]{2,1,0:T(8,128)(2,1)}), bf16[8,64,1024]{2,1,0:T(8,128)(2,1)S(1)}, u32[]{:S(2)}, u32[]{:S(2)}) async-start(bf16[8,64,1024]{2,1,0:T(8,128)(2,1)} %bitcast.8), calls=%async_computation.2 | async-start | bytes 2097152 | tf_op jit(solution)/shard_map/all_to_all | solution.py:212
Sparse Core Ops, SparseCore 0:
  11.9 64.9 all-gather.2
Sparse Core Ops, SparseCore 1:
  45.9 126.2 reduce-scatter.1
  201.2 59.8 all-gather.4
where the time goes:
time: 319 us; the launch traced here: 318 us
  waiting for transfers between devices  176 us (55%)
  matrix products  45.5 us (14%)
  Pallas kernels  32.4 us (10%)
  blocking collectives  19.4 us (6%)
  between operations  17.5 us (5%)
  other arithmetic  14.1 us (4%)
  local copies, waits for them, and re-layouts  6.85 us (2%)
  starting transfers between devices  5.82 us (2%)
    reduce_scatter x1, waiting for transfers between devices, local(): lax.psum_scatter(jnp.dot(columns, policy_weight, preferred_element_type=j...  80.1 us
    all_gather x1, waiting for transfers between devices, local(): segment = lax.all_gather(logit_grad, 'dp', axis=0, tiled=True)  59.9 us
    all_gather x1, waiting for transfers between devices, local(): lax.all_gather(reference_hidden, ('dp', 'vocab'), axis=0, tiled=True)  30.1 us
    all_to_all x1, blocking collectives, local(): lax.all_to_all(policy_hidden, 'dp', split_axis=1, concat_axis=0, tiled=True)  19.4 us
    pallas_call x1, Pallas kernels, grad_matmul(): pl.pallas_call(grad_kernel, grid=(width // tile,), in_specs=[pl.BlockSpec...  19 us
    dot_general x1, matrix products, local(): jnp.dot(columns, policy_weight, preferred_element_type=jnp.float32)  16 us
    dot_general x1, matrix products, local(): lax.dot_general(segment, policy_weight, (((1,), (1,)), ((), ())), preferr...  15.7 us
    dot_general x1, matrix products, local(): jnp.dot(lax.all_gather(reference_hidden, ('dp', 'vocab'), axis=0, tiled=T...  13.8 us
  transfers between devices with their start and end apart: 4, of which 4 were waited for; matrix products, arithmetic and copies ran while one was open for 11% of the time, Pallas kernels for 6%

commit v1 on v0

v1 whole, which is shorter than its diff:
```python
import functools

import jax
import jax.numpy as jnp
from jax import lax
from jax.experimental import pallas as pl
from jax.experimental.pallas import tpu as pltpu
from jax.sharding import PartitionSpec as P

SEQ_LEN = 32
CORES = 2
STEPS = 32767.0

beta = 0.1
loss_scale = 4096.0


def pair_terms(log_ratio, pair_index):
    chosen = pair_index[0::2]
    rejected = pair_index[1::2]
    numbers = jnp.arange(log_ratio.shape[0], dtype=jnp.int32)[:, None]
    is_chosen = numbers == chosen[None, :]
    is_rejected = numbers == rejected[None, :]
    signed = jnp.where(is_chosen, 1.0, 0.0) - jnp.where(is_rejected, 1.0, 0.0)
    margin = beta * jnp.sum(signed * log_ratio[:, None], axis=0)
    pair_count = chosen.shape[0]
    total_loss = jnp.sum(jax.nn.softplus(-margin)) / pair_count
    weight = -beta * loss_scale * jax.nn.sigmoid(-margin) / pair_count
    factor = jnp.sum(signed * weight[None, :], axis=1)
    return (total_loss, factor)


def greet(d, v, data_peers, vocab_peers):
    barrier = pltpu.get_barrier_semaphore()
    for peer in data_peers:
        pl.semaphore_signal(
            barrier, inc=1, device_id=(peer, v), device_id_type=pl.DeviceIdType.MESH
        )
    for peer in vocab_peers:
        pl.semaphore_signal(
            barrier, inc=1, device_id=(d, peer), device_id_type=pl.DeviceIdType.MESH
        )
    pl.semaphore_wait(barrier, len(data_peers) + len(vocab_peers))


def remote(source, target, send_sem, recv_sem, peer):
    return pltpu.make_async_remote_copy(
        src_ref=source,
        dst_ref=target,
        send_sem=send_sem,
        recv_sem=recv_sem,
        device_id=peer,
        device_id_type=pl.DeviceIdType.MESH,
    )


def exchange_bits(nd, nv):
    bits = []
    bit = CORES
    while bit < nd:
        bits.append(("dp", bit))
        bit *= 2
    bit = nv // 2
    while bit >= 1:
        bits.append(("vocab", bit))
        bit //= 2
    bits.append(("dp", 1))
    return bits


def row_order(bits, nd, nv):
    names = []
    bit = nd // 2
    while bit >= 1:
        names.append(("dp", bit))
        bit //= 2
    bit = nv // 2
    while bit >= 1:
        names.append(("vocab", bit))
        bit //= 2
    return [names.index(b) for b in reversed(bits)], len(names)


def flip(index, bit):
    return index + bit * (1 - 2 * ((index // bit) % 2))


def forward_kernel(
    nd, nv, pieces, tile, inside,
    hidden, w, ref_in, wr, policy_wanted, reference_wanted,
    logits, stats, cols,
    wbuf, dsend, drecv, xsend, xrecv, ssend, srecv, refh,
    own_sem, w_sem, wr_sem, a_send, a_recv, d_send, d_recv, x_send, x_recv, s_send, s_recv,
    r_own, r_send, r_recv,
):
    d, v = lax.axis_index("dp"), lax.axis_index("vocab")
    chips = nd // CORES
    chip, core = d // CORES, lax.rem(d, CORES)
    partner = chip * CORES + (1 - core)
    depth = wbuf.shape[1]
    tokens = refh.shape[0]
    away = (chips - 1) * pieces
    bits = exchange_bits(nd, nv) if inside else []
    vocab_peers = [flip(v, bit) for axis, bit in bits if axis == "vocab"]
    greet(d, v, [lax.rem(d + k, nd) for k in range(1, nd)], vocab_peers)

    def columns_of(peer):
        return hidden.at[:, pl.ds(pl.multiple_of(peer * depth, depth), depth)]

    moves = []
    for k in range(1, nd):
        peer = lax.rem(d + k, nd)
        move = remote(
            columns_of(peer), cols.at[d], a_send.at[k - 1], a_recv.at[k - 1], (peer, v)
        )
        move.start()
        moves.append(move)
    own_move = pltpu.make_async_copy(columns_of(d), cols.at[d], own_sem)
    own_move.start()

    place = 0
    if inside:
        for s, (axis, bit) in enumerate(bits):
            place = place + lax.rem((d if axis == "dp" else v) // bit, 2) * (2**s)
        per = tokens // (nd * nv)
        own_rows = refh.at[pl.ds(pl.multiple_of(place * per, per), per)]
        ref_move = pltpu.make_async_copy(ref_in, own_rows, r_own)
    else:
        ref_move = pltpu.make_async_copy(ref_in, refh, r_own)
    ref_move.start()

    def exchange(s):
        axis, bit = bits[s]
        size = per * 2**s
        rows = refh.at[pl.ds(pl.multiple_of((place // 2**s) * size, size), size)]
        peer = (flip(d, bit), v) if axis == "dp" else (d, flip(v, bit))
        return remote(rows, rows, r_send.at[s], r_recv.at[s], peer)

    def load(t):
        j = t // 2
        whose = lax.rem(t, 2) * core + (1 - lax.rem(t, 2)) * (1 - core)
        to = lax.rem(chip + j // pieces + 1, chips)
        at = ((to * CORES + whose) * pieces + lax.rem(j, pieces)) * tile
        return pltpu.make_async_copy(
            w.at[:, pl.ds(pl.multiple_of(at, tile), tile)], wbuf.at[t], w_sem.at[t]
        )

    def load_reference(m):
        return pltpu.make_async_copy(
            wr.at[
                pl.ds(pl.multiple_of(lax.rem(m, nd) * depth, depth), depth),
                pl.ds(pl.multiple_of((m // nd) * tile, tile), tile),
            ],
            wbuf.at[m],
            wr_sem.at[m],
        )

    def run(start, stop, step):
        lax.fori_loop(start, stop, lambda i, carry: (step(i), carry)[1], 0)

    run(0, nd * pieces, lambda t: load(t).start())
    ref_move.wait()
    if inside:
        exchange(0).start()
        exchange(0).wait()
        exchange(1).start()
    own_move.wait()
    for move in moves:
        move.wait()

    def product(t):
        load(t).wait()
        return jnp.dot(
            cols[...].reshape(tokens, depth), wbuf[t], preferred_element_type=jnp.float32
        )

    def to_partner(j):
        return remote(dsend.at[j], drecv.at[j], d_send.at[j], d_recv.at[j], (partner, v))

    def to_chip(j):
        peer = (lax.rem(chip + j // pieces + 1, chips) * CORES + core, v)
        return (
            remote(xsend.at[j], xrecv.at[j], x_send.at[j], x_recv.at[j], peer),
            remote(ssend.at[j], srecv.at[j], s_send.at[j], s_recv.at[j], peer),
        )

    def away_step(j):
        dsend[j] = product(2 * j)
        to_partner(j).start()
        part = product(2 * j + 1)
        to_partner(j).wait_recv()
        part = part + drecv[j]
        largest = jnp.maximum(jnp.max(jnp.abs(part)), 1e-30)
        xsend[j] = jnp.round(part * (STEPS / largest)).astype(jnp.int32).astype(jnp.int16)
        ssend[j] = jnp.full(ssend.shape[1:], 1.0 / STEPS, jnp.float32) * largest
        for copy in to_chip(j):
            copy.start()

    def home_step(n):
        dsend[away + n] = product(2 * (away + n))
        to_partner(away + n).start()
        logits[n] = product(2 * (away + n) + 1)

    first = min(1, away)
    run(0, first, away_step)
    if inside:
        exchange(1).wait()
        exchange(2).start()
    run(first, away, away_step)
    run(0, 2 * away, lambda m: load_reference(m).start())
    if inside:
        exchange(2).wait()
        exchange(3).start()
    run(0, pieces, home_step)
    run(2 * away, nd * pieces, lambda m: load_reference(m).start())
    if inside:
        for s in range(4, len(bits)):
            exchange(s - 1).wait()
            exchange(s).start()
        exchange(len(bits) - 1).wait()

    lanes = lax.broadcasted_iota(jnp.int32, (tokens, 128), 1)
    for half in range(2):
        stats[3 * half] = jnp.full((tokens, 128), -3e38, jnp.float32)
        stats[3 * half + 1] = jnp.zeros((tokens, 128), jnp.float32)
        stats[3 * half + 2] = jnp.zeros((tokens, 128), jnp.float32)

    def add_stats(half, value, wanted, n):
        parts = [value[:, g * 128 : (g + 1) * 128] for g in range(tile // 128)]
        before = stats[3 * half]
        top = functools.reduce(jnp.maximum, parts, before)
        total = stats[3 * half + 1] * jnp.exp(before - top)
        pick = stats[3 * half + 2]
        for g, part in enumerate(parts):
            total = total + jnp.exp(part - top)
            pick = pick + jnp.where(lanes + (n * tile + g * 128) == wanted[...], part, 0.0)
        stats[3 * half] = top
        stats[3 * half + 1] = total
        stats[3 * half + 2] = pick

    def reference_step(n):
        total = None
        for k in range(nd):
            load_reference(n * nd + k).wait()
            part = jnp.dot(
                refh[:, k * depth : (k + 1) * depth],
                wbuf[n * nd + k],
                preferred_element_type=jnp.float32,
            )
            total = part if total is None else total + part
        add_stats(1, total, reference_wanted, n)

    run(0, pieces, reference_step)

    def join_step(n):
        to_partner(away + n).wait_recv()
        total = logits[n] + drecv[away + n]
        for k in range(chips - 1):
            j = k * pieces + n
            for copy in to_chip(j):
                copy.wait_recv()
            total = total + xrecv[j].astype(jnp.int32).astype(jnp.float32) * srecv[j, 0:1, 0:1]
        logits[n] = total
        add_stats(0, total, policy_wanted, n)

    run(0, pieces, join_step)
    run(0, away + pieces, lambda j: to_partner(j).wait_send())

    def sent(j):
        for copy in to_chip(j):
            copy.wait_send()

    run(0, away, sent)


def forward(hidden, weight, reference_hidden, reference_weight, policy_wanted, reference_wanted):
    nd, nv = lax.axis_size("dp"), lax.axis_size("vocab")
    tokens = policy_wanted.shape[0]
    depth, width = weight.shape
    full = reference_weight.shape[0]
    block = width // nd
    tile = min(512, block)
    pieces = block // tile
    inside = reference_hidden.shape[0] < tokens
    away = max((nd // CORES - 1) * pieces, 1)
    hops = max(len(exchange_bits(nd, nv)), 1)
    count = nd * pieces
    half = count // 2
    hbm = pl.BlockSpec(memory_space=pl.ANY)
    vmem = pl.BlockSpec(memory_space=pltpu.VMEM)
    dma = pltpu.SemaphoreType.DMA
    f32, bf16 = jnp.float32, jnp.bfloat16
    return pl.pallas_call(
        functools.partial(forward_kernel, nd, nv, pieces, tile, inside),
        out_shape=[
            jax.ShapeDtypeStruct((pieces, tokens, tile), f32),
            jax.ShapeDtypeStruct((6, tokens, 128), f32),
            jax.ShapeDtypeStruct((nd, tokens // nd, depth), bf16),
        ],
        in_specs=[hbm, hbm, hbm, hbm, vmem, vmem],
        out_specs=[vmem, vmem, vmem],
        scratch_shapes=[
            pltpu.VMEM((count, depth, tile), bf16),
            pltpu.VMEM((half, tokens, tile), f32),
            pltpu.VMEM((half, tokens, tile), f32),
            pltpu.VMEM((away, tokens, tile), jnp.int16),
            pltpu.VMEM((away, tokens, tile), jnp.int16),
            pltpu.VMEM((away, 8, 128), f32),
            pltpu.VMEM((away, 8, 128), f32),
            pltpu.VMEM((tokens, full), bf16),
            dma,
            dma((count,)),
            dma((count,)),
            dma((nd - 1,)),
            dma((nd - 1,)),
            dma((half,)),
            dma((half,)),
            dma((away,)),
            dma((away,)),
            dma((away,)),
            dma((away,)),
            dma,
            dma((hops,)),
            dma((hops,)),
        ],
        compiler_params=pltpu.CompilerParams(
            collective_id=1, has_side_effects=True, vmem_limit_bytes=67043328
        ),
        name="forward",
    )(hidden, weight, reference_hidden, reference_weight, policy_wanted, reference_wanted)


def merge(parts, rows):
    tops = [part[:rows] for part in parts]
    top = functools.reduce(jnp.maximum, tops)
    total = sum(part[rows : 2 * rows] * jnp.exp(t - top) for part, t in zip(parts, tops))
    pick = sum(part[2 * rows : 3 * rows] for part in parts)
    return top, total, pick


def stats_kernel(
    nd, nv, rows, own, total_ref, ratio_ref, near, joined, far, send_d, recv_d, send_v, recv_v
):
    d, v = lax.axis_index("dp"), lax.axis_index("vocab")
    data_peers = [lax.rem(d + k, nd) for k in range(1, nd)]
    vocab_peers = [lax.rem(v + k, nv) for k in range(1, nv)]
    greet(d, v, data_peers, vocab_peers)
    copies = [
        remote(own, near.at[k], send_d.at[k], recv_d.at[k], (p, v))
        for k, p in enumerate(data_peers)
    ]
    for copy in copies:
        copy.start()
    for copy in copies:
        copy.wait()
    for half in range(2):
        span = slice(3 * half * rows, 3 * (half + 1) * rows)
        parts = merge([own[span]] + [near[k, span] for k in range(nd - 1)], rows)
        for k, value in enumerate(parts):
            joined[(3 * half + k) * rows : (3 * half + k + 1) * rows] = value
    copies = [
        remote(joined, far.at[k], send_v.at[k], recv_v.at[k], (d, p))
        for k, p in enumerate(vocab_peers)
    ]
    for copy in copies:
        copy.start()
    for copy in copies:
        copy.wait()
    logps = []
    for half in range(2):
        span = slice(3 * half * rows, 3 * (half + 1) * rows)
        top, total, pick = merge([joined[span]] + [far[k, span] for k in range(nv - 1)], rows)
        total = top + jnp.log(total)
        if half == 0:
            total_ref[...] = total
        logps.append(pick - total)
    ratio_ref[...] = logps[0] - logps[1]


def exchange_stats(stats):
    nd, nv = lax.axis_size("dp"), lax.axis_size("vocab")
    rows = stats.shape[0] // 6
    space = pl.BlockSpec(memory_space=pltpu.VMEM)
    return pl.pallas_call(
        functools.partial(stats_kernel, nd, nv, rows),
        out_shape=[jax.ShapeDtypeStruct((rows, 128), jnp.float32)] * 2,
        in_specs=[space],
        out_specs=[space] * 2,
        scratch_shapes=[
            pltpu.VMEM((nd - 1, 6 * rows, 128), jnp.float32),
            pltpu.VMEM((6 * rows, 128), jnp.float32),
            pltpu.VMEM((nv - 1, 6 * rows, 128), jnp.float32),
            pltpu.SemaphoreType.DMA((nd - 1,)),
            pltpu.SemaphoreType.DMA((nd - 1,)),
            pltpu.SemaphoreType.DMA((nv - 1,)),
            pltpu.SemaphoreType.DMA((nv - 1,)),
        ],
        compiler_params=pltpu.CompilerParams(collective_id=0, has_side_effects=True),
        name="exchange_stats",
    )(stats)


def backward_kernel(
    nd, nv, pieces, tile,
    g, w,
    others, hidden,
    wbuf, total, hsend, hrecv,
    w_sem, n_send, n_recv, x_send, x_recv, f_send, f_recv, h_send, h_recv,
):
    d, v = lax.axis_index("dp"), lax.axis_index("vocab")
    chips = nd // CORES
    chip, core = d // CORES, lax.rem(d, CORES)
    partner = chip * CORES + (1 - core)
    parts, sub = g.shape[1], g.shape[2]
    depth = wbuf.shape[1]
    tokens = nv * parts * sub
    greet(
        d,
        v,
        [lax.rem(d + k, nd) for k in range(1, nd)],
        [lax.rem(v + k, nv) for k in range(1, nv)],
    )

    def run(start, stop, step):
        lax.fori_loop(start, stop, lambda i, carry: (step(i), carry)[1], 0)

    def to_chip(k, n):
        peer = (lax.rem(chip + k, chips) * CORES + core, v)
        i = (k - 1) * parts + n
        return remote(
            g.at[:, n], others.at[2 * k - 1, :, n], x_send.at[i], x_recv.at[i], peer
        )

    def to_partner(k, n):
        i = (k - 1) * parts + n
        return remote(
            others.at[2 * k - 1, :, n],
            others.at[2 * k, :, n],
            f_send.at[i],
            f_recv.at[i],
            (partner, v),
        )

    for n in range(parts):
        for k in range(1, chips):
            to_chip(k, n).start()
    near = remote(g, others.at[0], n_send, n_recv, (partner, v))
    near.start()

    def load(t):
        slot = t // pieces
        whose = lax.rem(slot, 2) * (1 - core) + (1 - lax.rem(slot, 2)) * core
        back = slot // 2
        to = lax.rem(chip - back + chips, chips)
        at = ((to * CORES + whose) * pieces + lax.rem(t, pieces)) * tile
        return pltpu.make_async_copy(
            w.at[:, pl.ds(pl.multiple_of(at, tile), tile)], wbuf.at[t], w_sem.at[t]
        )

    run(0, nd * pieces, lambda t: load(t).start())

    def product(piece, t):
        return lax.dot_general(
            piece, wbuf[t], (((1,), (1,)), ((), ())), preferred_element_type=jnp.float32
        )

    def cut(t):
        at = lax.rem(t, pieces) * tile
        return pl.ds(pl.multiple_of(at, tile), tile)

    total[...] = jnp.zeros_like(total)

    def own_step(t):
        load(t).wait()
        piece = g[:, :, :, cut(t)].reshape(tokens, tile)
        total[...] += product(piece, t).reshape(total.shape)

    def near_step(t):
        load(t).wait()
        piece = others[0, :, :, :, cut(t)].reshape(tokens, tile)
        total[...] += product(piece, t).reshape(total.shape)

    run(0, pieces, own_step)
    near.wait()
    run(pieces, 2 * pieces, near_step)
    run(2 * pieces, nd * pieces, lambda t: load(t).wait())

    def to_vocab(n, k):
        peer = lax.rem(v + k, nv)
        i = n * (nv - 1) + k - 1
        return remote(hsend.at[n, peer], hrecv.at[n, k - 1], h_send.at[i], h_recv.at[i], (d, peer))

    def add_piece(slot, n, t):
        piece = others[slot, :, n, :, cut(t)].reshape(nv * sub, tile)
        return product(piece, t)

    def part_step(n):
        for k in range(1, chips):
            to_chip(k, n).wait_recv()
            to_partner(k, n).start()
        value = total[:, n].reshape(nv * sub, depth)
        for k in range(1, chips):
            for p in range(pieces):
                value = value + add_piece(2 * k - 1, n, 2 * k * pieces + p)
        for k in range(1, chips):
            to_partner(k, n).wait_recv()
            for p in range(pieces):
                value = value + add_piece(2 * k, n, (2 * k + 1) * pieces + p)
        hsend[n] = value.astype(jnp.bfloat16).reshape(nv, sub, depth)
        for k in range(1, nv):
            to_vocab(n, k).start()

    run(0, parts, part_step)

    def sum_step(n):
        value = hsend[n, v].astype(jnp.float32)
        for k in range(1, nv):
            to_vocab(n, k).wait_recv()
            value = value + hrecv[n, k - 1].astype(jnp.float32)
        hidden[n] = value.astype(hidden.dtype)

    run(0, parts, sum_step)

    def sent(n):
        for k in range(1, chips):
            to_chip(k, n).wait_send()
            to_partner(k, n).wait_send()
        for k in range(1, nv):
            to_vocab(n, k).wait_send()

    run(0, parts, sent)


def backward(g, weight):
    nd, nv = lax.axis_size("dp"), lax.axis_size("vocab")
    tokens, block = g.shape
    depth = weight.shape[0]
    tile = min(512, block)
    pieces = block // tile
    group = tokens // nv
    sub = 16 if group % 16 == 0 else group
    parts = group // sub
    moves = max((nd // CORES - 1) * parts, 1)
    dma = pltpu.SemaphoreType.DMA
    vmem = pl.BlockSpec(memory_space=pltpu.VMEM)
    others, hidden = pl.pallas_call(
        functools.partial(backward_kernel, nd, nv, pieces, tile),
        out_shape=[
            jax.ShapeDtypeStruct((nd - 1, nv, parts, sub, block), jnp.bfloat16),
            jax.ShapeDtypeStruct((parts, sub, depth), jnp.bfloat16),
        ],
        in_specs=[vmem, pl.BlockSpec(memory_space=pl.ANY)],
        out_specs=[vmem, vmem],
        scratch_shapes=[
            pltpu.VMEM((nd * pieces, depth, tile), jnp.bfloat16),
            pltpu.VMEM((nv, parts, sub, depth), jnp.float32),
            pltpu.VMEM((parts, nv, sub, depth), jnp.bfloat16),
            pltpu.VMEM((parts, nv - 1, sub, depth), jnp.bfloat16),
            dma((nd * pieces,)),
            dma,
            dma,
            dma((moves,)),
            dma((moves,)),
            dma((moves,)),
            dma((moves,)),
            dma((parts * (nv - 1),)),
            dma((parts * (nv - 1),)),
        ],
        compiler_params=pltpu.CompilerParams(
            collective_id=2, has_side_effects=True, vmem_limit_bytes=67043328
        ),
        name="backward",
    )(g.reshape(nv, parts, sub, block), weight)
    return others.reshape(nd - 1, tokens, block), hidden.reshape(group, depth)


def weight_kernel(steps, at_ref, rows_ref, own_ref, others_ref, out_ref):
    i = pl.program_id(0)

    @pl.when(i < steps)
    def _():
        out_ref[...] = jnp.dot(
            rows_ref[...], own_ref[...], preferred_element_type=jnp.float32
        ).astype(out_ref.dtype)

    @pl.when(i >= steps)
    def _():
        out_ref[...] = jnp.dot(
            rows_ref[...], others_ref[0], preferred_element_type=jnp.float32
        ).astype(out_ref.dtype)


def weight_matmul(rows_t, own, others, slot_columns, width):
    depth, tokens = rows_t.shape
    block = own.shape[1]
    tile = min(1024, block)
    steps = block // tile
    count = others.shape[0] + 1
    at = jnp.concatenate(
        [
            (column // tile).astype(jnp.int32) + jnp.arange(steps, dtype=jnp.int32)
            for column in slot_columns
        ]
    )
    return pl.pallas_call(
        functools.partial(weight_kernel, steps),
        grid_spec=pltpu.PrefetchScalarGridSpec(
            num_scalar_prefetch=1,
            grid=(steps * count,),
            in_specs=[
                pl.BlockSpec((depth, tokens), lambda i, at: (0, 0)),
                pl.BlockSpec((tokens, tile), lambda i, at: (0, jnp.minimum(i, steps - 1))),
                pl.BlockSpec(
                    (1, tokens, tile),
                    lambda i, at: (
                        jnp.maximum(i // steps - 1, 0),
                        0,
                        jnp.where(i < steps, 0, lax.rem(i, steps)),
                    ),
                ),
            ],
            out_specs=pl.BlockSpec((depth, tile), lambda i, at: (0, at[i])),
        ),
        out_shape=jax.ShapeDtypeStruct((depth, width), jnp.bfloat16),
        cost_estimate=pl.CostEstimate(
            flops=2 * depth * tokens * width,
            bytes_accessed=2 * (depth * tokens + tokens * width + depth * width),
            transcendentals=0,
        ),
        name="weight_grad",
    )(at, rows_t, own, others)


def local(
    policy_hidden,
    policy_weight,
    reference_hidden,
    reference_weight,
    targets,
    response_mask,
    pair_index,
):
    d = lax.axis_index("dp")
    v = lax.axis_index("vocab")
    nd = lax.axis_size("dp")
    nv = lax.axis_size("vocab")
    chip, core = d // CORES, d % CORES
    chips = nd // CORES
    tokens = targets.shape[0]
    width = policy_weight.shape[1]
    block = width // nd

    bits = exchange_bits(nd, nv)
    order, count = row_order(bits, nd, nv)
    fold = (2,) * count + (-1,)
    inverse = [order.index(k) for k in range(count)]
    inside = reference_hidden.shape[0] % 16 == 0 and len(bits) >= 4
    reference_targets = targets - (d * nv + v) * reference_weight.shape[1]
    if inside:
        reference_targets = reference_targets.reshape(fold).transpose(*order, count).reshape(-1)
    else:
        reference_hidden = lax.all_gather(reference_hidden, ("dp", "vocab"), axis=0, tiled=True)
    base = v * width + d * block
    own_targets = targets - base

    def lanes(x):
        return jnp.broadcast_to(x[:, None], (tokens, 128))

    logits, stats, rows = forward(
        policy_hidden,
        policy_weight,
        reference_hidden,
        reference_weight,
        lanes(own_targets),
        lanes(reference_targets),
    )
    rows = rows.reshape(tokens, -1)
    packed = []
    for half in range(2):
        tops = stats[3 * half]
        top = jnp.max(tops, axis=1)
        total = jnp.sum(stats[3 * half + 1] * jnp.exp(tops - top[:, None]), axis=1)
        pick = jnp.sum(stats[3 * half + 2], axis=1)
        for stat in (top, total, pick):
            if half == 1 and inside:
                stat = stat.reshape(fold).transpose(*inverse, count).reshape(-1)
            packed.append(stat.reshape(-1, 128))
    totals, ratio = exchange_stats(jnp.concatenate(packed))
    active = response_mask.astype(jnp.float32)
    log_ratio = jnp.sum((active * ratio.reshape(-1)).reshape(-1, SEQ_LEN), axis=1)
    total_loss, factor = pair_terms(log_ratio, pair_index)
    scale = active * jnp.repeat(factor, SEQ_LEN)
    policy_total = totals.reshape(-1)

    logits = jnp.concatenate([logits[n] for n in range(logits.shape[0])], axis=1)
    column_ids = lax.broadcasted_iota(jnp.int32, logits.shape, 1)
    onehot = (column_ids == own_targets[:, None]).astype(jnp.float32)
    grad = (scale[:, None] * (onehot - jnp.exp(logits - policy_total[:, None]))).astype(
        jnp.bfloat16
    )
    others, hidden_grad = backward(grad, policy_weight)
    columns = [d * block, (chip * CORES + 1 - core) * block]
    for k in range(1, chips):
        back = (chip - k + chips) % chips
        columns += [(back * CORES + core) * block, (back * CORES + 1 - core) * block]
    weight_grad = weight_matmul(rows.T, grad, others, columns, width)
    return (hidden_grad, weight_grad, total_loss)


def solution(mesh):
    placed = (
        P("dp", None),
        P("dp", "vocab"),
        P(("dp", "vocab"), None),
        P(None, ("dp", "vocab")),
        P(),
        P(),
        P(),
    )
    return jax.shard_map(
        local,
        mesh=mesh,
        in_specs=placed,
        out_specs=(P("vocab", "dp"), P("dp", "vocab"), P()),
        check_vma=False,
    )
```

time: 319 us -> 214 us (0.67)
  waiting for transfers between devices: 176 us -> 0 us
  Pallas kernels: 32.4 us -> 184 us
  matrix products: 45.5 us -> 0 us
  blocking collectives: 19.4 us -> 0 us
  between operations: 17.5 us -> 2.74 us
  local copies, waits for them, and re-layouts: 6.85 us -> 14.9 us
  starting transfers between devices: 5.82 us -> 0 us
    pallas_call x2 -> x4, Pallas kernels: 32.4 us -> 184 us  [the longest x1 93.3 us: forward(): pl.pallas_call(functools.partial(forward_kernel, nd, nv, pieces, tile, in...]
    all_gather x2 -> x0, waiting for transfers between devices: 90 us -> none  [the longest x1 59.9 us: local(): segment = lax.all_gather(logit_grad, 'dp', axis=0, tiled=True)]
    reduce_scatter x1 -> x0, waiting for transfers between devices: 80.1 us -> none  [local(): lax.psum_scatter(jnp.dot(columns, policy_weight, preferred_element_type=j...]
    dot_general x3 -> x0, matrix products: 45.5 us -> none  [the longest x1 16 us: local(): jnp.dot(columns, policy_weight, preferred_element_type=jnp.float32)]
    all_to_all x1 -> x0, blocking collectives: 19.4 us -> none  [local(): lax.all_to_all(policy_hidden, 'dp', split_axis=1, concat_axis=0, tiled=True)]
    all_to_all x1 -> x0, starting transfers between devices: 5.52 us -> none  [local(): lax.all_to_all(hidden_piece.astype(jnp.bfloat16).reshape(vocab_devices, -...]
    all_to_all x1 -> x0, waiting for transfers between devices: 5.46 us -> none  [local(): lax.all_to_all(hidden_piece.astype(jnp.bfloat16).reshape(vocab_devices, -...]
    squeeze x0 -> x1, local copies, waits for them, and re-layouts: none -> 3.24 us  [local(): logits[n]]
  transfers between devices with their start and end apart: 4 -> 0, of which waited for: 4 -> 0; matrix products, arithmetic and copies ran while one was open for 11% -> 0% of each run, Pallas kernels for 6% -> 0%
where the time goes in v1:
time: 214 us
  Pallas kernels  184 us (86%)
  local copies, waits for them, and re-layouts  14.9 us (7%)
  other arithmetic  11.9 us (6%)
  between operations  2.74 us (1%)
    pallas_call x1, Pallas kernels, forward(): pl.pallas_call(functools.partial(forward_kernel, nd, nv, pieces, tile, in...  93.3 us
    pallas_call x1, Pallas kernels, backward(): pl.pallas_call(functools.partial(backward_kernel, nd, nv, pieces, tile),...  63.6 us
    pallas_call x1, Pallas kernels, weight_matmul(): pl.pallas_call(functools.partial(weight_kernel, steps), grid_spec=pltpu.P...  16.4 us
    pallas_call x1, Pallas kernels, exchange_stats(): pl.pallas_call(functools.partial(stats_kernel, nd, nv, rows), out_shape=[...  10.9 us
    convert_element_type x2, other arithmetic, local(): (scale[:, None] * (onehot - jnp.exp(logits - policy_total[:, None]))).ast...  5.8 us

profile of v1, /device:TPU:0, one launch (start us, length us, event | category | flops | bytes accessed | tf_op | source)
XLA Modules:
  0.0 213.8 jit_solution(16876596302938680123)
XLA Ops:
  0.8 0.7 pad_add_fusion.at_ref
  1.4 1.3 slice.37
  2.7 1.3 slice.36
  4.0 0.7 broadcast_subtract_fusion
  4.7 0.0 copy-start.2
  4.7 0.1 reshape.85
  4.8 0.1 broadcast_in_dim.38
  4.9 0.7 eq.50
  5.6 0.8 broadcast_in_dim.39.reference_wanted
  6.4 0.0 copy-done.2
  6.4 0.8 broadcast_in_dim.20.policy_wanted
  7.3 93.3 %forward.1 = (f32[4,512,512]{2,1,0:T(8,128)}, f32[6,512,128]{2,1,0:T(8,128)}, bf16[4,128,1024]{2,1,0:T(8,128)(2,1)}) custom-call(bf16[128,4096]{1,0:T(8,128)(2,1)} %hidden.1, bf16[1024,8192]{1,0:T(8,128)(2,1)} %w.3, bf16[16,4096]{1,0:T(8,128)(2,1)} %ref_in.1, bf16[4096,2048]{1,0:T(8,128)(2,1)} %wr.1, s32[512,128]{1,0:T(8,128)} %broadcast_in_dim.20.policy_wanted, ...), custom_call_target="tpu_custom_call" | custom-call | tf_op jit(solution)/shard_map/forward/pallas_call | solution.py:293
  100.6 0.0 copy-start.5
  100.6 0.0 copy-start.6
  100.6 0.0 copy-start.7
  100.6 2.4 %copy.25 = bf16[512,1024]{0,1:T(8,128)(2,1)} copy(bf16[512,1024]{1,0:T(8,128)(2,1)} %bitcast.51) | data formatting | bytes 2097152 | tf_op jit(solution)/shard_map/reshape | solution.py:677
  103.0 1.5 slice_reduce_fusion
  104.5 1.6 fusion.10
  106.1 0.1 reshape.91
  106.2 0.1 reshape_reshape.11
  106.3 0.1 reshape.90
  106.4 0.1 reshape_reshape.10
  106.5 0.1 reshape.89
  106.6 0.1 reshape_reshape.9
  106.7 1.8 concatenate.20.own
  108.5 10.9 %exchange_stats.1 = (f32[4,128]{1,0:T(4,128)}, f32[4,128]{1,0:T(4,128)}) custom-call(f32[24,128]{1,0:T(8,128)} %concatenate.20.own), custom_call_target="tpu_custom_call" | custom-call | tf_op jit(solution)/shard_map/exchange_stats/pallas_call | solution.py:384
  119.4 0.0 copy-done.5
  119.5 0.7 bitcast_multiply_fusion
  120.1 0.1 reshape.93
  120.2 0.1 reduce_sum.76
  120.3 0.0 copy-done.6
  120.3 0.0 copy-done.7
  120.3 0.2 multiply_reduce_fusion.1
  120.5 0.6 fusion.14
  121.8 0.1 multiply_reduce_fusion
  121.9 0.1 broadcast_in_dim.40
  122.0 0.1 reshape.94
  122.1 0.1 mul.94
  122.1 0.8 sub.86
  122.9 0.0 copy-start.3
  122.9 0.0 copy-start.4
  122.9 3.2 %slice_bitcast_fusion.3 = (f32[512,512]{1,0:T(8,128)S(1)}, f32[512,512]{1,0:T(8,128)S(1)}, f32[512,512]{1,0:T(8,128)S(1)}, f32[512,512]{1,0:T(8,128)S(1)}, f32[1...) fusion(f32[4,512,512]{2,1,0:T(8,128)} %get-tuple-element.12), kind=kLoop, calls=%fused_computation.44 | loop fusion | bytes 12582912 | tf_op jit(solution)/shard_map/squeeze | solution.py:695
  126.2 0.0 copy-start.1
  126.2 0.0 copy-done.3
  126.2 0.0 copy-done.4
  126.2 3.0 %fusion.7.own_ref = bf16[512,2048]{1,0:T(8,128)(2,1)} fusion(f32[512,512]{1,0:T(8,128)S(1)} %get-tuple-element.26, f32[512,512]{1,0:T(8,128)S(1)} %get-tuple-element.25, f32[512,512]{1,0:T(8,128)S(1)} %get-tuple-element.24, f32[512,512]{1,0:T(8,128)S(1)} %get-tuple-element.23, f32[512]{0:T(512)S(1)} %bitcast.58, s32[512]{0:T(512)S(1)} %copy-done.3, ...), kind=kLoop, calls=%fused_computation.9 | loop fusion | flops 9437184 | bytes 6297600 | tf_op jit(solution)/shard_map/convert_element_type | solution.py:698
  129.2 0.0 copy-done.1
  129.2 2.8 %fusion.3.g = bf16[8,4,16,2048]{3,2,1,0:T(8,128)(2,1)} fusion(f32[8,4,16,512]{3,2,1,0:T(8,128)S(1)} %bitcast.46, f32[8,4,16,512]{3,2,1,0:T(8,128)S(1)} %bitcast.47, f32[8,4,16,512]{3,2,1,0:T(8,128)S(1)} %bitcast.48, f32[8,4,16,512]{3,2,1,0:T(8,128)S(1)} %bitcast.49, f32[8,4,16]{2,1,0:T(4,128)S(1)} %sub.86, s32[8,4,16]{2,1,0:T(4,128)S(1)} %copy-done.1, ...), kind=kLoop, calls=%fused_computation.4 | loop fusion | flops 9437184 | bytes 6297600 | tf_op jit(solution)/shard_map/convert_element_type | solution.py:698
  132.0 63.6 %backward.1 = (bf16[3,8,4,16,2048]{4,3,2,1,0:T(8,128)(2,1)}, bf16[4,16,1024]{2,1,0:T(8,128)(2,1)}) custom-call(bf16[8,4,16,2048]{3,2,1,0:T(8,128)(2,1)} %fusion.3.g, bf16[1024,8192]{1,0:T(8,128)(2,1)} %w.3), custom_call_target="tpu_custom_call" | custom-call | tf_op jit(solution)/shard_map/backward/pallas_call | solution.py:546
  195.6 0.0 copy-start
  195.6 16.4 %weight_grad.1 = bf16[1024,8192]{1,0:T(8,128)(2,1)} custom-call(s32[8]{0:T(128)} %pad_add_fusion.at_ref, bf16[1024,512]{1,0:T(8,128)(2,1)} %bitcast.50, bf16[512,2048]{1,0:T(8,128)(2,1)} %fusion.7.own_ref, bf16[3,512,2048]{2,1,0:T(8,128)(2,1)} %bitcast.61), custom_call_target="tpu_custom_call" | custom-call | flops 8589934592 | bytes 26214400 | tf_op jit(solution)/shard_map/weight_grad/pallas_call | solution.py:605
  212.0 0.0 copy-done
  212.0 0.7 copy.27
  (7 shorter events, 0.1 us)
Async XLA Ops:
  4.7 1.8 copy-start.2
  100.6 18.9 %copy-start.5 = (s32[512]{0:T(512)S(1)}, s32[512]{0:T(512)}, u32[]{:S(2)}) copy-start(s32[512]{0:T(512)} %param.12) | copy-start | bytes 6148
  100.6 19.8 %copy-start.6 = (s32[8]{0:T(128)S(1)}, s32[8]{0:T(128)}, u32[]{:S(2)}) copy-start(s32[8]{0:T(128)} %slice.37) | copy-start | bytes 100
  100.6 19.7 %copy-start.7 = (s32[8]{0:T(128)S(1)}, s32[8]{0:T(128)}, u32[]{:S(2)}) copy-start(s32[8]{0:T(128)} %slice.36) | copy-start | bytes 100
  122.9 3.3 %copy-start.3 = (s32[512]{0:T(512)S(1)}, s32[512]{0:T(512)}, u32[]{:S(2)}) copy-start(s32[512]{0:T(512)} %copy-done.2) | copy-start | bytes 6148
  122.9 3.3 %copy-start.4 = (f32[4,128]{1,0:T(4,128)S(1)}, f32[4,128]{1,0:T(4,128)}, u32[]{:S(2)}) copy-start(f32[4,128]{1,0:T(4,128)} %get-tuple-element.13) | copy-start | bytes 6148
  126.2 3.0 %copy-start.1 = (s32[8,4,16]{2,1,0:T(4,128)S(1)}, s32[8,4,16]{2,1,0:T(4,128)}, u32[]{:S(2)}) copy-start(s32[8,4,16]{2,1,0:T(4,128)} %eq.50) | copy-start | bytes 6148
  195.6 16.4 %copy-start = (bf16[4,16,1024]{2,1,0:T(8,128)(2,1)S(1)}, bf16[4,16,1024]{2,1,0:T(8,128)(2,1)}, u32[]{:S(2)}) copy-start(bf16[4,16,1024]{2,1,0:T(8,128)(2,1)} %get-tuple-element.14) | copy-start | bytes 393220

commit v2 on v1

v2 whole, which is shorter than its diff:
```python
import functools

import jax
import jax.numpy as jnp
from jax import lax
from jax.experimental import pallas as pl
from jax.experimental.pallas import tpu as pltpu
from jax.sharding import PartitionSpec as P

SEQ_LEN = 32
CORES = 2
STEPS = 32767.0

beta = 0.1
loss_scale = 4096.0


def greet(d, v, data_peers, vocab_peers):
    barrier = pltpu.get_barrier_semaphore()
    for peer in data_peers:
        pl.semaphore_signal(
            barrier, inc=1, device_id=(peer, v), device_id_type=pl.DeviceIdType.MESH
        )
    for peer in vocab_peers:
        pl.semaphore_signal(
            barrier, inc=1, device_id=(d, peer), device_id_type=pl.DeviceIdType.MESH
        )
    pl.semaphore_wait(barrier, len(data_peers) + len(vocab_peers))


def remote(source, target, send_sem, recv_sem, peer):
    return pltpu.make_async_remote_copy(
        src_ref=source,
        dst_ref=target,
        send_sem=send_sem,
        recv_sem=recv_sem,
        device_id=peer,
        device_id_type=pl.DeviceIdType.MESH,
    )


def exchange_bits(nd, nv):
    bits = []
    bit = CORES
    while bit < nd:
        bits.append(("dp", bit))
        bit *= 2
    bit = nv // 2
    while bit >= 1:
        bits.append(("vocab", bit))
        bit //= 2
    bits.append(("dp", 1))
    return bits


def flip(index, bit):
    return index + bit * (1 - 2 * ((index // bit) % 2))


def merge(parts, rows):
    tops = [part[:rows] for part in parts]
    top = functools.reduce(jnp.maximum, tops)
    total = sum(part[rows : 2 * rows] * jnp.exp(t - top) for part, t in zip(parts, tops))
    pick = sum(part[2 * rows : 3 * rows] for part in parts)
    return top, total, pick


def head_kernel(
    nd, nv, pieces, tile, inside, pairs,
    hidden, w, ref_in, wr, numbers, pair_row,
    g, others, hidden_out, cols, loss,
    wbuf, dsend, drecv, xsend, xrecv, ssend, srecv, refh, logits, stats, marks,
    packed, near_stats, joined, far_stats, total_grad, hsend, hrecv,
    own_sem, w_sem, wr_sem, a_send, a_recv, d_send, d_recv, x_send, x_recv, s_send, s_recv,
    r_own, r_send, r_recv, sd_send, sd_recv, sv_send, sv_recv,
    b_sem, n_send, n_recv, gx_send, gx_recv, f_send, f_recv, h_send, h_recv,
):
    d, v = lax.axis_index("dp"), lax.axis_index("vocab")
    chips = nd // CORES
    chip, core = d // CORES, lax.rem(d, CORES)
    partner = chip * CORES + (1 - core)
    depth = wbuf.shape[1]
    tokens = refh.shape[0]
    away = (chips - 1) * pieces
    parts, sub = g.shape[1], g.shape[2]
    rows = tokens // 128
    bits = exchange_bits(nd, nv) if inside else []
    data_peers = [lax.rem(d + k, nd) for k in range(1, nd)]
    vocab_peers = [lax.rem(v + k, nv) for k in range(1, nv)]
    greet(d, v, data_peers, vocab_peers)

    place = 0
    if inside:
        for s, (axis, bit) in enumerate(bits):
            place = place + lax.rem((d if axis == "dp" else v) // bit, 2) * (2**s)
        per = tokens // (nd * nv)
        own_rows = refh.at[pl.ds(pl.multiple_of(place * per, per), per)]
        ref_move = pltpu.make_async_copy(ref_in, own_rows, r_own)
    else:
        ref_move = pltpu.make_async_copy(ref_in, refh, r_own)
    ref_move.start()

    def exchange(s):
        axis, bit = bits[s]
        size = per * 2**s
        rows = refh.at[pl.ds(pl.multiple_of((place // 2**s) * size, size), size)]
        peer = (flip(d, bit), v) if axis == "dp" else (d, flip(v, bit))
        return remote(ref_in if s == 0 else rows, rows, r_send.at[s], r_recv.at[s], peer)

    if inside:
        exchange(0).start()

    def columns_of(peer):
        return hidden.at[:, pl.ds(pl.multiple_of(peer * depth, depth), depth)]

    moves = []
    for k in range(1, nd):
        peer = lax.rem(d + k, nd)
        move = remote(
            columns_of(peer), cols.at[d], a_send.at[k - 1], a_recv.at[k - 1], (peer, v)
        )
        move.start()
        moves.append(move)
    own_move = pltpu.make_async_copy(columns_of(d), cols.at[d], own_sem)
    own_move.start()

    def load(t):
        j = t // 2
        whose = lax.rem(t, 2) * core + (1 - lax.rem(t, 2)) * (1 - core)
        to = lax.rem(chip + j // pieces + 1, chips)
        at = ((to * CORES + whose) * pieces + lax.rem(j, pieces)) * tile
        return pltpu.make_async_copy(
            w.at[:, pl.ds(pl.multiple_of(at, tile), tile)], wbuf.at[t], w_sem.at[t]
        )

    def load_reference(m):
        return pltpu.make_async_copy(
            wr.at[
                pl.ds(pl.multiple_of(lax.rem(m, nd) * depth, depth), depth),
                pl.ds(pl.multiple_of((m // nd) * tile, tile), tile),
            ],
            wbuf.at[m],
            wr_sem.at[m],
        )

    def run(start, stop, step):
        lax.fori_loop(start, stop, lambda i, carry: (step(i), carry)[1], 0)

    run(0, nd * pieces, lambda t: load(t).start())

    lanes = lax.broadcasted_iota(jnp.int32, (tokens, 128), 1)
    lines = lax.broadcasted_iota(jnp.int32, (tokens, 128), 0)
    named = lines
    if inside:
        named = lax.rem(lines, per)
        for s, (axis, bit) in enumerate(bits):
            step = bit * (nv if axis == "dp" else 1) * per
            named = named + lax.rem(lines // (per * 2**s), 2) * step

    def to_column(at, names):
        total = None
        for k in range(rows):
            row = numbers[at + k : at + k + 1].astype(jnp.float32)
            part = jnp.where(names == lanes + k * 128, row, 0.0)
            total = part if total is None else total + part
        return jnp.sum(total, axis=1, keepdims=True)

    def row_to_column(value):
        total = None
        for k in range(rows):
            part = jnp.where(lines == lanes + k * 128, value[k : k + 1], 0.0)
            total = part if total is None else total + part
        return jnp.sum(total, axis=1, keepdims=True)

    def to_rows(column, names, at):
        for k in range(rows):
            packed[at + k : at + k + 1] = jnp.sum(
                jnp.where(names == lanes + k * 128, column, 0.0), axis=0, keepdims=True
            )

    base = v * (nd * pieces * tile) + d * (pieces * tile)
    reference_base = (d * nv + v) * (pieces * tile)
    wanted = to_column(0, lines).astype(jnp.int32) - base
    marks[0] = jnp.broadcast_to(wanted, (tokens, 128)).reshape(marks.shape[1:])
    wanted = to_column(0, named).astype(jnp.int32) - reference_base
    marks[1] = jnp.broadcast_to(wanted, (tokens, 128)).reshape(marks.shape[1:])
    ref_move.wait()
    if inside:
        exchange(0).wait()
        exchange(1).start()
    own_move.wait()
    for move in moves:
        move.wait()

    def product(t):
        load(t).wait()
        return jnp.dot(
            cols[...].reshape(tokens, depth), wbuf[t], preferred_element_type=jnp.float32
        )

    def to_partner(j):
        source = dsend.at[lax.rem(j, pieces)]
        return remote(source, drecv.at[j], d_send.at[j], d_recv.at[j], (partner, v))

    def send_partner(j):
        @pl.when(j >= pieces)
        def _():
            to_partner(j - pieces).wait_send()

        dsend[lax.rem(j, pieces)] = product(2 * j)
        to_partner(j).start()

    def to_chip(j):
        peer = (lax.rem(chip + j // pieces + 1, chips) * CORES + core, v)
        return (
            remote(xsend.at[j], xrecv.at[j], x_send.at[j], x_recv.at[j], peer),
            remote(ssend.at[j], srecv.at[j], s_send.at[j], s_recv.at[j], peer),
        )

    def away_step(j):
        send_partner(j)
        part = product(2 * j + 1)
        to_partner(j).wait_recv()
        part = part + drecv[j]
        largest = jnp.maximum(jnp.max(jnp.abs(part)), 1e-30)
        xsend[j] = jnp.round(part * (STEPS / largest)).astype(jnp.int32).astype(jnp.int16)
        ssend[j] = jnp.full(ssend.shape[1:], 1.0 / STEPS, jnp.float32) * largest
        for copy in to_chip(j):
            copy.start()

    def home_step(n):
        send_partner(away + n)
        logits[n] = product(2 * (away + n) + 1).reshape(logits.shape[1:])

    late = max(away - 1, 0)
    if inside:
        exchange(1).wait()
        exchange(2).start()
    run(0, late, away_step)
    if inside:
        exchange(2).wait()
        exchange(3).start()
    run(late, away, away_step)
    run(0, 2 * away, lambda m: load_reference(m).start())
    run(0, pieces, home_step)
    run(2 * away, nd * pieces, lambda m: load_reference(m).start())

    for half in range(2):
        stats[3 * half] = jnp.full((tokens, 128), -3e38, jnp.float32)
        stats[3 * half + 1] = jnp.zeros((tokens, 128), jnp.float32)
        stats[3 * half + 2] = jnp.zeros((tokens, 128), jnp.float32)

    def add_stats(half, value, n):
        wanted = marks[half].reshape(tokens, 128)
        cuts = [value[:, i * 128 : (i + 1) * 128] for i in range(tile // 128)]
        before = stats[3 * half]
        top = functools.reduce(jnp.maximum, cuts, before)
        total = stats[3 * half + 1] * jnp.exp(before - top)
        pick = stats[3 * half + 2]
        for i, part in enumerate(cuts):
            total = total + jnp.exp(part - top)
            pick = pick + jnp.where(lanes + (n * tile + i * 128) == wanted, part, 0.0)
        stats[3 * half] = top
        stats[3 * half + 1] = total
        stats[3 * half + 2] = pick

    def join_step(n):
        to_partner(away + n).wait_recv()
        total = logits[n].reshape(tokens, tile) + drecv[away + n]
        for k in range(chips - 1):
            j = k * pieces + n
            for copy in to_chip(j):
                copy.wait_recv()
            total = total + xrecv[j].astype(jnp.int32).astype(jnp.float32) * srecv[j, 0:1, 0:1]
        logits[n] = total.reshape(logits.shape[1:])
        add_stats(0, total, n)

    run(0, pieces // 2, join_step)
    if inside:
        for s in range(4, len(bits)):
            exchange(s - 1).wait()
            exchange(s).start()
    run(pieces // 2, pieces - 1, join_step)
    if inside:
        exchange(len(bits) - 1).wait()

    def reference_step(n):
        total = None
        for k in range(nd):
            load_reference(n * nd + k).wait()
            part = jnp.dot(
                refh[:, k * depth : (k + 1) * depth],
                wbuf[n * nd + k],
                preferred_element_type=jnp.float32,
            )
            total = part if total is None else total + part
        add_stats(1, total, n)

    def pack_stats(half, names):
        tops = stats[3 * half]
        top = jnp.max(tops, axis=1, keepdims=True)
        total = jnp.sum(stats[3 * half + 1] * jnp.exp(tops - top), axis=1, keepdims=True)
        pick = jnp.sum(stats[3 * half + 2], axis=1, keepdims=True)
        for i, column in enumerate((top, total, pick)):
            to_rows(column, names, (3 * half + i) * rows)

    run(0, pieces, reference_step)

    def load_again(t):
        slot = t // pieces
        whose = lax.rem(slot, 2) * (1 - core) + (1 - lax.rem(slot, 2)) * core
        to = lax.rem(chip - slot // 2 + chips, chips)
        at = ((to * CORES + whose) * pieces + lax.rem(t, pieces)) * tile
        return pltpu.make_async_copy(
            w.at[:, pl.ds(pl.multiple_of(at, tile), tile)], wbuf.at[t], b_sem.at[t]
        )

    run(0, nd * pieces, lambda t: load_again(t).start())
    pack_stats(1, named)

    run(pieces - 1, pieces, join_step)
    pack_stats(0, lines)

    copies = [
        remote(packed, near_stats.at[k], sd_send.at[k], sd_recv.at[k], (p, v))
        for k, p in enumerate(data_peers)
    ]
    for copy in copies:
        copy.start()
    for copy in copies:
        copy.wait()
    for half in range(2):
        span = slice(3 * half * rows, 3 * (half + 1) * rows)
        merged = merge([packed[span]] + [near_stats[k, span] for k in range(nd - 1)], rows)
        for i, value in enumerate(merged):
            joined[(3 * half + i) * rows : (3 * half + i + 1) * rows] = value
    copies = [
        remote(joined, far_stats.at[k], sv_send.at[k], sv_recv.at[k], (d, p))
        for k, p in enumerate(vocab_peers)
    ]
    for copy in copies:
        copy.start()
    for copy in copies:
        copy.wait()
    logps = []
    for half in range(2):
        span = slice(3 * half * rows, 3 * (half + 1) * rows)
        top, total, pick = merge([joined[span]] + [far_stats[k, span] for k in range(nv - 1)], rows)
        total = top + jnp.log(total)
        if half == 0:
            policy_total = row_to_column(total)
        logps.append(pick - total)
    ratio = row_to_column(logps[0] - logps[1])

    active = to_column(rows, lines)
    member = jnp.where(lines // SEQ_LEN == pair_row[0:1], active, 0.0)
    log_ratio = jnp.sum(member * ratio, axis=0, keepdims=True)
    log_ratio = jnp.broadcast_to(log_ratio, (8, 128))
    lane = lax.broadcasted_iota(jnp.int32, (8, 128), 1)
    even = lax.rem(lane, 2) == 0
    mate = jnp.where(even, pltpu.roll(log_ratio, 127, 1), pltpu.roll(log_ratio, 1, 1))
    margin = beta * jnp.where(even, log_ratio - mate, mate - log_ratio)
    lost = jnp.maximum(-margin, 0.0) + jnp.log1p(jnp.exp(-jnp.abs(margin)))
    lost = jnp.where(even & (lane < 2 * pairs), lost, 0.0)
    loss[...] = jnp.broadcast_to(jnp.sum(lost, axis=1, keepdims=True) / pairs, (8, 128))
    chance = 1.0 / (1.0 + jnp.exp(jnp.minimum(margin, 80.0)))
    factor = jnp.where(even, -beta, beta) * loss_scale * chance / pairs
    scale = jnp.sum(member * factor[0:1], axis=1, keepdims=True)
    stats[0] = jnp.broadcast_to(policy_total, (tokens, 128))
    stats[1] = jnp.broadcast_to(scale, (tokens, 128))

    def grad_to_chip(k, n):
        peer = (lax.rem(chip + k, chips) * CORES + core, v)
        i = (k - 1) * parts + n
        return remote(g.at[:, n], others.at[2 * k - 1, :, n], gx_send.at[i], gx_recv.at[i], peer)

    def forward_on(k, n):
        i = (k - 1) * parts + n
        return remote(
            others.at[2 * k - 1, :, n],
            others.at[2 * k, :, n],
            f_send.at[i],
            f_recv.at[i],
            (partner, v),
        )

    part_lanes = lax.broadcasted_iota(jnp.int32, (nv, sub, 128), 2)
    by_part = (nv, parts, sub, 128)
    for n in range(parts):
        whole = stats[0].reshape(by_part)[:, n]
        size = stats[1].reshape(by_part)[:, n]
        mark = marks[0, :, n]
        for p in range(pieces):
            for i in range(tile // 128):
                value = jnp.exp(logits[p, :, n, :, i * 128 : (i + 1) * 128] - whole)
                hit = jnp.where(part_lanes + (p * tile + i * 128) == mark, 1.0, 0.0)
                at = p * tile + i * 128
                g[:, n, :, at : at + 128] = (size * (hit - value)).astype(g.dtype)
        for k in range(1, chips):
            grad_to_chip(k, n).start()
    near = remote(g, others.at[0], n_send, n_recv, (partner, v))
    near.start()

    def hidden_product(piece, t):
        return lax.dot_general(
            piece, wbuf[t], (((1,), (1,)), ((), ())), preferred_element_type=jnp.float32
        )

    def cut(t):
        return pl.ds(pl.multiple_of(lax.rem(t, pieces) * tile, tile), tile)

    total_grad[...] = jnp.zeros_like(total_grad)

    def own_step(t):
        load_again(t).wait()
        piece = g[:, :, :, cut(t)].reshape(tokens, tile)
        total_grad[...] += hidden_product(piece, t).reshape(total_grad.shape)

    def near_step(t):
        load_again(t).wait()
        piece = others[0, :, :, :, cut(t)].reshape(tokens, tile)
        total_grad[...] += hidden_product(piece, t).reshape(total_grad.shape)

    run(0, pieces, own_step)
    near.wait()
    run(pieces, 2 * pieces, near_step)
    run(2 * pieces, nd * pieces, lambda t: load_again(t).wait())

    def to_vocab(n, k):
        peer = lax.rem(v + k, nv)
        i = n * (nv - 1) + k - 1
        return remote(hsend.at[n, peer], hrecv.at[n, k - 1], h_send.at[i], h_recv.at[i], (d, peer))

    def add_piece(slot, n, p, t):
        piece = others[slot, :, n, :, p * tile : (p + 1) * tile].reshape(nv * sub, tile)
        return hidden_product(piece, t)

    def part_step(n):
        for k in range(1, chips):
            grad_to_chip(k, n).wait_recv()
            forward_on(k, n).start()
        value = total_grad[:, n].reshape(nv * sub, depth)
        for k in range(1, chips):
            for p in range(pieces):
                value = value + add_piece(2 * k - 1, n, p, 2 * k * pieces + p)
        for k in range(1, chips):
            forward_on(k, n).wait_recv()
            for p in range(pieces):
                value = value + add_piece(2 * k, n, p, (2 * k + 1) * pieces + p)
        hsend[n] = value.astype(jnp.bfloat16).reshape(nv, sub, depth)
        for k in range(1, nv):
            to_vocab(n, k).start()

    run(0, parts, part_step)

    def sum_step(n):
        value = hsend[n, v].astype(jnp.float32)
        for k in range(1, nv):
            to_vocab(n, k).wait_recv()
            value = value + hrecv[n, k - 1].astype(jnp.float32)
        hidden_out[n] = value.astype(hidden_out.dtype)

    run(0, parts, sum_step)

    def part_sent(n):
        for k in range(1, chips):
            grad_to_chip(k, n).wait_send()
            forward_on(k, n).wait_send()
        for k in range(1, nv):
            to_vocab(n, k).wait_send()

    run(0, parts, part_sent)
    run(away, away + pieces, lambda j: to_partner(j).wait_send())

    def sent(j):
        for copy in to_chip(j):
            copy.wait_send()

    run(0, away, sent)


def head(hidden, weight, reference_hidden, reference_weight, targets, mask, pair_index):
    nd, nv = lax.axis_size("dp"), lax.axis_size("vocab")
    tokens = targets.shape[0]
    depth, width = weight.shape
    full = reference_weight.shape[0]
    block = width // nd
    tile = min(512, block)
    pieces = block // tile
    rows = tokens // 128
    group = tokens // nv
    sub = 16 if group % 16 == 0 else group
    parts = group // sub
    inside = reference_hidden.shape[0] < tokens
    away = max((nd // CORES - 1) * pieces, 1)
    hops = max(len(exchange_bits(nd, nv)), 1)
    moves = max((nd // CORES - 1) * parts, 1)
    count = nd * pieces
    half = count // 2
    hbm = pl.BlockSpec(memory_space=pl.ANY)
    vmem = pl.BlockSpec(memory_space=pltpu.VMEM)
    dma = pltpu.SemaphoreType.DMA
    f32, bf16 = jnp.float32, jnp.bfloat16
    numbers = jnp.concatenate([targets, mask]).reshape(2 * rows, 128)
    pairs = pair_index.shape[0] // 2
    pair_row = jnp.pad(pair_index, (0, 128 - 2 * pairs), constant_values=-1)
    pair_row = jnp.broadcast_to(pair_row[None], (8, 128))
    g, others, hidden_grad, cols, loss = pl.pallas_call(
        functools.partial(head_kernel, nd, nv, pieces, tile, inside, pairs),
        out_shape=[
            jax.ShapeDtypeStruct((nv, parts, sub, block), bf16),
            jax.ShapeDtypeStruct((nd - 1, nv, parts, sub, block), bf16),
            jax.ShapeDtypeStruct((parts, sub, depth), bf16),
            jax.ShapeDtypeStruct((nd, tokens // nd, depth), bf16),
            jax.ShapeDtypeStruct((8, 128), f32),
        ],
        in_specs=[hbm, hbm, hbm, hbm, vmem, vmem],
        out_specs=[vmem] * 5,
        scratch_shapes=[
            pltpu.VMEM((count, depth, tile), bf16),
            pltpu.VMEM((pieces, tokens, tile), f32),
            pltpu.VMEM((half, tokens, tile), f32),
            pltpu.VMEM((away, tokens, tile), jnp.int16),
            pltpu.VMEM((away, tokens, tile), jnp.int16),
            pltpu.VMEM((away, 8, 128), f32),
            pltpu.VMEM((away, 8, 128), f32),
            pltpu.VMEM((tokens, full), bf16),
            pltpu.VMEM((pieces, nv, parts, sub, tile), f32),
            pltpu.VMEM((6, tokens, 128), f32),
            pltpu.VMEM((2, nv, parts, sub, 128), jnp.int32),
            pltpu.VMEM((6 * rows, 128), f32),
            pltpu.VMEM((nd - 1, 6 * rows, 128), f32),
            pltpu.VMEM((6 * rows, 128), f32),
            pltpu.VMEM((nv - 1, 6 * rows, 128), f32),
            pltpu.VMEM((nv, parts, sub, depth), f32),
            pltpu.VMEM((parts, nv, sub, depth), bf16),
            pltpu.VMEM((parts, nv - 1, sub, depth), bf16),
            dma,
            dma((count,)),
            dma((count,)),
            dma((nd - 1,)),
            dma((nd - 1,)),
            dma((half,)),
            dma((half,)),
            dma((away,)),
            dma((away,)),
            dma((away,)),
            dma((away,)),
            dma,
            dma((hops,)),
            dma((hops,)),
            dma((nd - 1,)),
            dma((nd - 1,)),
            dma((nv - 1,)),
            dma((nv - 1,)),
            dma((count,)),
            dma,
            dma,
            dma((moves,)),
            dma((moves,)),
            dma((moves,)),
            dma((moves,)),
            dma((parts * (nv - 1),)),
            dma((parts * (nv - 1),)),
        ],
        compiler_params=pltpu.CompilerParams(
            collective_id=0, has_side_effects=True, vmem_limit_bytes=67043328
        ),
        name="head",
    )(hidden, weight, reference_hidden, reference_weight, numbers, pair_row)
    return (
        g.reshape(tokens, block),
        others.reshape(nd - 1, tokens, block),
        hidden_grad.reshape(group, depth),
        cols.reshape(tokens, depth),
        loss[0, 0],
    )


def weight_kernel(steps, at_ref, rows_ref, own_ref, others_ref, out_ref):
    i = pl.program_id(0)

    def product(g):
        return lax.dot_general(
            rows_ref[...], g, (((0,), (0,)), ((), ())), preferred_element_type=jnp.float32
        ).astype(out_ref.dtype)

    @pl.when(i < steps)
    def _():
        out_ref[...] = product(own_ref[...])

    @pl.when(i >= steps)
    def _():
        out_ref[...] = product(others_ref[0])


def weight_matmul(rows, own, others, slot_columns, width):
    tokens, depth = rows.shape
    block = own.shape[1]
    tile = min(1024, block)
    steps = block // tile
    count = others.shape[0] + 1
    at = jnp.concatenate(
        [
            (column // tile).astype(jnp.int32) + jnp.arange(steps, dtype=jnp.int32)
            for column in slot_columns
        ]
    )
    return pl.pallas_call(
        functools.partial(weight_kernel, steps),
        grid_spec=pltpu.PrefetchScalarGridSpec(
            num_scalar_prefetch=1,
            grid=(steps * count,),
            in_specs=[
                pl.BlockSpec((tokens, depth), lambda i, at: (0, 0)),
                pl.BlockSpec((tokens, tile), lambda i, at: (0, jnp.minimum(i, steps - 1))),
                pl.BlockSpec(
                    (1, tokens, tile),
                    lambda i, at: (
                        jnp.maximum(i // steps - 1, 0),
                        0,
                        jnp.where(i < steps, 0, lax.rem(i, steps)),
                    ),
                ),
            ],
            out_specs=pl.BlockSpec((depth, tile), lambda i, at: (0, at[i])),
        ),
        out_shape=jax.ShapeDtypeStruct((depth, width), jnp.bfloat16),
        cost_estimate=pl.CostEstimate(
            flops=2 * depth * tokens * width,
            bytes_accessed=2 * (depth * tokens + tokens * width + depth * width),
            transcendentals=0,
        ),
        name="weight_grad",
    )(at, rows, own, others)


def local(
    policy_hidden,
    policy_weight,
    reference_hidden,
    reference_weight,
    targets,
    response_mask,
    pair_index,
):
    d = lax.axis_index("dp")
    v = lax.axis_index("vocab")
    nd = lax.axis_size("dp")
    nv = lax.axis_size("vocab")
    chip, core = d // CORES, d % CORES
    chips = nd // CORES
    width = policy_weight.shape[1]
    block = width // nd
    if reference_hidden.shape[0] % 16 != 0 or len(exchange_bits(nd, nv)) < 4:
        reference_hidden = lax.all_gather(reference_hidden, ("dp", "vocab"), axis=0, tiled=True)
    grad, others, hidden_grad, rows, total_loss = head(
        policy_hidden,
        policy_weight,
        reference_hidden,
        reference_weight,
        targets,
        response_mask,
        pair_index,
    )
    columns = [d * block, (chip * CORES + 1 - core) * block]
    for k in range(1, chips):
        back = (chip - k + chips) % chips
        columns += [(back * CORES + core) * block, (back * CORES + 1 - core) * block]
    weight_grad = weight_matmul(rows, grad, others, columns, width)
    return (hidden_grad, weight_grad, total_loss)


def solution(mesh):
    placed = (
        P("dp", None),
        P("dp", "vocab"),
        P(("dp", "vocab"), None),
        P(None, ("dp", "vocab")),
        P(),
        P(),
        P(),
    )
    return jax.shard_map(
        local,
        mesh=mesh,
        in_specs=placed,
        out_specs=(P("vocab", "dp"), P("dp", "vocab"), P()),
        check_vma=False,
    )
```

time: 214 us -> 167 us (0.78)
  Pallas kernels: 184 us -> 161 us
  local copies, waits for them, and re-layouts: 14.9 us -> 3.14 us
  other arithmetic: 11.9 us -> 1.91 us
    pallas_call x3 -> x1, Pallas kernels: 168 us -> 145 us  [head(): pl.pallas_call(functools.partial(head_kernel, nd, nv, pieces, tile, insid...]
    convert_element_type x2 -> x0, other arithmetic: 5.8 us -> none  [local(): (scale[:, None] * (onehot - jnp.exp(logits - policy_total[:, None]))).ast...]
    reduce_sum x6 -> x0, other arithmetic: 4.1 us -> none  [the longest x1 1.55 us: local(): total = jnp.sum(stats[3 * half + 1] * jnp.exp(tops - top[:, None]), axis=1)]
    squeeze x1 -> x0, local copies, waits for them, and re-layouts: 3.24 us -> none  [local(): logits[n]]
    reshape x7 -> x0, local copies, waits for them, and re-layouts: 2.87 us -> none  [the longest x1 2.36 us: local(): rows = rows.reshape(tokens, -1)]
where the time goes in v2:
time: 167 us
  Pallas kernels  161 us (96%)
  local copies, waits for them, and re-layouts  3.14 us (2%)
  other arithmetic  1.91 us (1%)
    pallas_call x1, Pallas kernels, head(): pl.pallas_call(functools.partial(head_kernel, nd, nv, pieces, tile, insid...  145 us
    pallas_call x1, Pallas kernels, weight_matmul(): pl.pallas_call(functools.partial(weight_kernel, steps), grid_spec=pltpu.P...  16.4 us

profile of v2, /device:TPU:0, one launch (start us, length us, event | category | flops | bytes accessed | tf_op | source)
XLA Modules:
  0.0 166.9 jit_solution(3941005141670511159)
XLA Ops:
  0.8 0.6 pad_add_fusion.1.at_ref
  1.4 0.7 pad.4
  2.0 0.6 broadcast_in_dim.2.pair_row
  2.6 1.3 pad_add_fusion.numbers
  3.9 144.6 %head.1 = (bf16[8,4,16,2048]{3,2,1,0:T(8,128)(2,1)}, bf16[3,8,4,16,2048]{4,3,2,1,0:T(8,128)(2,1)}, bf16[4,16,1024]{2,1,0:T(8,128)(2,1)}, bf16[4,128,1024]{2,1,0:T(8,128)(2,1)}, f32[8,128]{1,0:T(8,128)}) custom-call(bf16[128,4096]{1,0:T(8,128)(2,1)} %hidden.1, bf16[1024,8192]{1,0:T(8,128)(2,1)} %w.1, bf16[16,4096]{1,0:T(8,128)(2,1)} %ref_in.1, ...), custom_call_target="tpu_custom_call" | custom-call | tf_op jit(solution)/shard_map/head/pallas_call | solution.py:508
  148.5 0.0 copy-start
  148.5 1.2 slice.3
  149.8 16.4 %weight_grad.1 = bf16[1024,8192]{1,0:T(8,128)(2,1)} custom-call(s32[8]{0:T(128)} %pad_add_fusion.1.at_ref, bf16[512,1024]{1,0:T(8,128)(2,1)} %bitcast.12, bf16[512,2048]{1,0:T(8,128)(2,1)} %bitcast.11, bf16[3,512,2048]{2,1,0:T(8,128)(2,1)} %bitcast.10), custom_call_target="tpu_custom_call" | custom-call | flops 8589934592 | bytes 26214400 | tf_op jit(solution)/shard_map/weight_grad/pallas_call | solution.py:609
  166.2 0.0 copy-done
  166.2 0.7 copy.11
  (2 shorter events, 0.0 us)
Async XLA Ops:
  148.5 17.7 %copy-start = (bf16[4,16,1024]{2,1,0:T(8,128)(2,1)S(1)}, bf16[4,16,1024]{2,1,0:T(8,128)(2,1)}, u32[]{:S(2)}) copy-start(bf16[4,16,1024]{2,1,0:T(8,128)(2,1)} %get-tuple-element.8) | copy-start | bytes 393220
